TPU v7x, 32 devices: a 4x4x1 block of a 4x4x8 slice. The times are simulated.
32 devices in a mesh: dp: 1 (over z), fsdp: 4 (over y), ep: 8 (over x, core).
Axes of the slice: x: 4, y: 4, z: 1, core: 2. Of those that a mesh axis runs over, the one named last changes fastest.
The devices are a block of a 4x4x8 slice.
Arguments:
- hidden: bfloat16 [131072, 1024], P(('dp', 'fsdp', 'ep'))
- norm_gain: bfloat16 [1024], replicated
- w_router: bfloat16 [1024, 32], replicated
- w_gate: bfloat16 [32, 1024, 2816], P('ep', 'fsdp')
- w_up: bfloat16 [32, 1024, 2816], P('ep', 'fsdp')
- w_down: bfloat16 [32, 2816, 1024], P('ep', None, 'fsdp')
- top2_ids: int32 [131072, 2], P(('dp', 'fsdp', 'ep'))
Outputs:
- output: bfloat16 [131072, 1024], P(('dp', 'fsdp', 'ep'))
All inputs are finite; a program needn't handle non-finite values.
Results may differ from a plain program's by a relative error of at most 0.001.
Values are sent between devices in bfloat16 or wider.
A program may use at most 768 MiB of HBM per device.

v0:
```python
import jax
import jax.numpy as jnp
from jax import lax
from jax.sharding import PartitionSpec as P

EPS = 1e-5


def norm_and_gates(hidden, norm_gain, w_router, top2_ids):
    hidden_f32 = hidden.astype(jnp.float32)
    mean_sq = jnp.mean(hidden_f32 * hidden_f32, axis=-1, keepdims=True)
    normed = (hidden_f32 * lax.rsqrt(mean_sq + EPS) * norm_gain.astype(jnp.float32)).astype(jnp.bfloat16)
    logits = jnp.dot(normed, w_router, preferred_element_type=jnp.float32)
    gate_probs = jax.nn.softmax(jnp.take_along_axis(logits, top2_ids, axis=1), axis=-1)
    return hidden_f32, normed, gate_probs


def route_slots(top2_ids, num_experts, capacity):
    flat_ids = top2_ids.reshape(-1)
    onehot = (flat_ids[:, None] == jnp.arange(num_experts, dtype=jnp.int32)[None, :]).astype(jnp.int32)
    position = jnp.sum((jnp.cumsum(onehot, axis=0) - 1) * onehot, axis=1)
    slot_ids = jnp.where(position < capacity, flat_ids * capacity + position, num_experts * capacity)
    return slot_ids.reshape(top2_ids.shape)


def gather_rows(normed, slot_ids, num_slots):
    tok_count = slot_ids.shape[0]
    token_index = jnp.broadcast_to(jnp.arange(tok_count, dtype=jnp.int32)[:, None], slot_ids.shape)
    source = jnp.full((num_slots,), tok_count, dtype=jnp.int32).at[slot_ids.reshape(-1)].set(token_index.reshape(-1), mode='drop')
    return jnp.take(normed, source, axis=0, mode='fill', fill_value=0)


def take_slots(expert_rows, slot_ids):
    return jnp.take(expert_rows, slot_ids, axis=0, mode='fill', fill_value=0)


def expert_block(rows_in, gate_full, up_full, down_full):
    act_a = jnp.einsum('ecd,edf->ecf', rows_in, gate_full, preferred_element_type=jnp.float32)
    act_b = jnp.einsum('ecd,edf->ecf', rows_in, up_full, preferred_element_type=jnp.float32)
    hidden_act = (jax.nn.silu(act_a) * act_b).astype(jnp.bfloat16)
    return jnp.einsum('ecf,efd->ecd', hidden_act, down_full, preferred_element_type=jnp.float32).astype(jnp.bfloat16)


def local_block(hidden, norm_gain, w_router, w_gate, w_up, w_down, top2_ids):
    tok_local, d_model = hidden.shape
    num_experts = w_router.shape[1]
    capacity = (5 * tok_local + 2 * num_experts - 1) // (2 * num_experts)
    hidden_f32, normed, gate_probs = norm_and_gates(hidden, norm_gain, w_router, top2_ids)
    slot_ids = route_slots(top2_ids, num_experts, capacity)
    send_rows = gather_rows(normed, slot_ids, num_experts * capacity).reshape(num_experts, capacity, d_model)
    gate_full = lax.all_gather(w_gate, 'fsdp', axis=1, tiled=True)
    up_full = lax.all_gather(w_up, 'fsdp', axis=1, tiled=True)
    down_full = lax.all_gather(w_down, 'fsdp', axis=2, tiled=True)
    recv_rows = lax.all_to_all(send_rows, 'ep', 0, 1, tiled=True)
    expert_out = expert_block(recv_rows, gate_full, up_full, down_full)
    back_rows = lax.all_to_all(expert_out, 'ep', 1, 0, tiled=True)
    returned = take_slots(back_rows.reshape(num_experts * capacity, d_model), slot_ids)
    moe_sum = jnp.sum(gate_probs[:, :, None] * returned.astype(jnp.float32), axis=1)
    return (hidden_f32 + moe_sum).astype(jnp.bfloat16)


def solution(mesh):
    tok_spec = P(('dp', 'fsdp', 'ep'), None)
    in_specs = (tok_spec, P(None), P(None, None), P('ep', 'fsdp', None), P('ep', 'fsdp', None), P('ep', None, 'fsdp'), tok_spec)
    return jax.shard_map(local_block, mesh=mesh, in_specs=in_specs, out_specs=tok_spec, check_vma=False)
```

profile of v0, /device:TPU:97, one launch (start us, length us, event | category | flops | bytes accessed | tf_op | source)
XLA Modules:
  0.0 1159.2 jit_solution(5327496985190982385)
XLA Ops:
  6.6 0.7 all-gather.4.cloned.1.call-update
  7.4 0.7 all-gather.6.cloned.1.call-update
  8.1 1.4 copy.35
  9.5 1.2 eq.29
  10.7 1.2 eq.25
  12.1 9.5 reduce-window.6
  21.6 0.9 slice_reduce_fusion
  22.5 0.2 reduce-window.9
  22.8 0.6 copy.40
  23.4 1.4 mul.59
  25.0 1.2 reshape.148
  26.2 0.3 add_add_fusion
  26.6 0.8 fusion.5
  27.4 0.5 copy-done.5
  27.9 30.9 %scatter_custom_fusion = s32[10240]{0:T(1024)S(1)} fusion(s32[8192]{0:T(1024)S(1)} %bitcast.51, s32[8192]{0:T(1024)S(1)} %reshape.148, s32[]{:T(128)} %constant.68.clone.1), kind=kCustom, calls=%fused_computation.36 | custom fusion | bytes 40964 | tf_op jit(solution)/shard_map/scatter | solution.py:29
  59.0 5.1 fusion
  64.1 7.8 fusion.2
  72.0 55.0 %gather_fusion = bf16[10240,1024]{1,0:T(8,128)(2,1)} fusion(bf16[4096,1024]{1,0:T(8,128)(2,1)} %fusion.2, s32[10240]{0:T(1024)S(1)} %fusion.7), kind=kCustom, calls=%fused_computation | custom fusion | bytes 41984000 | tf_op jit(solution)/shard_map/jit(_take)/gather | solution.py:30
  127.0 17.6 %broadcast_select_fusion.1 = bf16[32,320,1024]{2,1,0:T(8,128)(2,1)} fusion(bf16[32,320,1024]{2,1,0:T(8,128)(2,1)} %bitcast.45, pred[32,320]{1,0:T(8,128)(4,1)S(1)} %broadcast_in_dim.58), kind=kLoop, calls=%fused_computation.10 | loop fusion | flops 10485760 | bytes 41953280 | tf_op jit(solution)/shard_map/jit(_take)/select_n | solution.py:30
  144.6 8.0 all-to-all-start
  152.6 0.7 all-gather.8.cloned.1.call-update
  153.4 227.7 %all-to-all-done = bf16[32,320,1024]{2,1,0:T(8,128)(2,1)} async-done(((bf16[32,320,1024]{2,1,0:T(8,128)(2,1)}), bf16[32,320,1024]{2,1,0:T(8,128)(2,1)}, u32[]{:S(2)}, u32[]{:S(2)}) %all-to-all-start) | async-done | bytes 20971552 | tf_op jit(solution)/shard_map/all_to_all | solution.py:54
  381.0 17.5 %copy.41 = bf16[4,8,320,1024]{3,2,1,0:T(8,128)(2,1)} copy(bf16[4,8,320,1024]{3,2,0,1:T(8,128)(2,1)} %bitcast.6) | data formatting | bytes 41943040 | tf_op jit(solution)/shard_map/all_to_all | solution.py:54
  398.6 74.1 %fusion.15 = f32[4,2560,2816]{2,1,0:T(8,128)} fusion(bf16[4,2560,1024]{2,1,0:T(8,128)(2,1)} %bitcast.46, bf16[4,1024,2816]{2,1,0:T(8,128)(2,1)} %all-gather.4.cloned.1.call-done), kind=kOutput, calls=%fused_computation.46 | convolution fusion | flops 59055800320 | bytes 159383552 | tf_op jit(solution)/shard_map/ecd,edf->ecf/dot_general | solution.py:38
  472.6 86.3 %multiply_convert_fusion.clone.4 = bf16[4,2560,2816]{2,1,0:T(8,128)(2,1)} fusion(f32[4,2560,2816]{2,1,0:T(8,128)} %fusion.15, bf16[4,2560,1024]{2,1,0:T(8,128)(2,1)} %bitcast.47, bf16[4,1024,2816]{2,1,0:T(8,128)(2,1)} %all-gather.6.cloned.1.call-done), kind=kOutput, calls=%fused_computation.4.clone.clone.clone.1 | convolution fusion | flops 59228815360 | bytes 217055232 | tf_op jit(solution)/shard_map/ecd,edf->ecf/dot_general | solution.py:39
  558.9 72.8 %all-gather.8.cloned.1.call-done = bf16[4,2816,1024]{2,1,0:T(8,128)(2,1)} async-done(((bf16[4,2816,256]{2,1,0:T(8,128)(2,1)}), bf16[4,2816,1024]{2,1,0:T(8,128)(2,1)}) %all-gather.8.cloned.1.call-update) | async-done | bytes 23068688 | tf_op jit(solution)/shard_map/all_gather | solution.py:53
  631.7 69.8 %convolution_convert_fusion = bf16[4,2560,1024]{2,1,0:T(8,128)(2,1)} fusion(bf16[4,2816,1024]{2,1,0:T(8,128)(2,1)} %all-gather.8.cloned.1.call-done, bf16[4,2560,2816]{2,1,0:T(8,128)(2,1)} %multiply_convert_fusion.clone.4), kind=kOutput, calls=%fused_computation.11 | convolution fusion | flops 59066286080 | bytes 101711872 | tf_op jit(solution)/shard_map/ecf,efd->ecd/dot_general | solution.py:41
  701.5 27.1 %copy.42 = bf16[4,2560,1024]{2,0,1:T(4,128)(2,1)} copy(bf16[4,2560,1024]{2,1,0:T(8,128)(2,1)} %convolution_convert_fusion) | data formatting | bytes 41943040 | tf_op jit(solution)/shard_map/convert_element_type | solution.py:41
  728.6 8.6 all-to-all-start.1
  737.2 2.1 reduce_sum.43
  739.3 0.6 copy.37
  739.9 0.7 compare_and_fusion
  740.6 0.6 copy.44
  741.2 1.8 reshape.132
  743.1 0.6 copy.32
  743.8 1.2 reshape.138
  745.0 5.9 fusion.14
  750.9 65.5 %gather_fusion.2 = f32[8192]{0:T(1024)S(1)} fusion(f32[4096,32]{0,1:T(8,128)S(1)} %fusion.14, s32[8192]{0:T(1024)S(1)} %reshape.138), kind=kCustom, calls=%fused_computation.2 | custom fusion | bytes 131072 | tf_op jit(solution)/shard_map/jit(take_along_axis)/gather | solution.py:14
  816.5 2.1 reshape.141
  818.6 0.6 copy.33
  819.4 0.6 copy.34
  820.1 0.8 copy.39
  820.9 144.5 %all-to-all-done.1 = bf16[4,2560,1024]{2,0,1:T(4,128)(2,1)} async-done(((bf16[4,2560,1024]{2,0,1:T(4,128)(2,1)}), bf16[4,2560,1024]{2,0,1:T(4,128)(2,1)}, u32[]{:S(2)}, u32[]{:S(2)}) %all-to-all-start.1) | async-done | bytes 20971552 | tf_op jit(solution)/shard_map/all_to_all | solution.py:56
  965.5 21.2 %copy.43 = bf16[4,8,320,1024]{3,2,0,1:T(8,128)(2,1)} copy(bf16[4,8,320,1024]{3,0,2,1:T(4,128)(2,1)} %bitcast.8) | data formatting | bytes 41943040 | tf_op jit(solution)/shard_map/all_to_all | solution.py:56
  986.7 50.3 %gather_fusion.1 = bf16[8192,1024]{1,0:T(8,128)(2,1)} fusion(bf16[10240,1024]{1,0:T(8,128)(2,1)} %bitcast.44, s32[8192]{0:T(1024)S(1)} %broadcast_clamp_fusion), kind=kCustom, calls=%fused_computation.1 | custom fusion | bytes 33587200 | tf_op jit(solution)/shard_map/jit(_take)/gather | solution.py:34
  1037.0 24.9 %reshape.131 = bf16[4096,2,1024]{2,1,0:T(2,128)(2,1)} reshape(bf16[8192,1024]{1,0:T(8,128)(2,1)} %gather_fusion.1) | data formatting | bytes 33554432 | tf_op jit(solution)/shard_map/jit(_take)/gather | solution.py:34
  1061.9 78.3 %multiply_reduce_fusion = f32[4096,1024]{1,0:T(8,128)} fusion(bf16[4096,2,1024]{2,1,0:T(2,128)(2,1)} %reshape.131, pred[4096,2]{1,0:T(8,128)(4,1)S(1)} %copy.39, f32[4096,2]{1,0:T(8,128)S(1)} %copy.34), kind=kLoop, calls=%fused_computation.5 | loop fusion | flops 29360128 | bytes 33595392 | tf_op jit(solution)/shard_map/reduce_sum | solution.py:58
  1140.3 12.0 %fusion.3 = bf16[4096,1024]{1,0:T(8,128)(2,1)} fusion(f32[4096,1024]{1,0:T(8,128)} %multiply_reduce_fusion, bf16[4096,1024]{1,0:T(8,128)(2,1)} %param.7), kind=kLoop, calls=%fused_computation.15 | loop fusion | flops 12582912 | bytes 33554432 | tf_op jit(solution)/shard_map/convert_element_type | solution.py:59
  (38 shorter events, 0.8 us)
Async XLA Ops:
  6.5 738.4 %copy-start = (bf16[1024,32]{0,1:T(8,128)(2,1)S(1)}, bf16[1024,32]{0,1:T(8,128)(2,1)}, u32[]{:S(2)}) copy-start(bf16[1024,32]{0,1:T(8,128)(2,1)} %param.9) | copy-start | bytes 196612
  6.6 16.2 %copy-start.2 = (s32[4096,2]{0,1:T(2,128)S(1)}, s32[4096,2]{0,1:T(2,128)}, u32[]{:S(2)}) copy-start(s32[4096,2]{0,1:T(2,128)} %param.13) | copy-start | bytes 98308
  6.6 19.7 %copy-start.9 = (bf16[1024]{0:T(1024)(128)(2,1)S(1)}, bf16[1024]{0:T(1024)(128)(2,1)}, u32[]{:S(2)}) copy-start(bf16[1024]{0:T(1024)(128)(2,1)} %param.8) | copy-start | bytes 6148
  6.6 392.0 %all-gather.4.cloned.1.call-start = ((), (), s32[]{:S(2)}) async-start(), calls=%async_computation.2 | async-start | bytes 28835840 | tf_op jit(solution)/shard_map/all_gather | solution.py:51
  7.3 465.3 %all-gather.6.cloned.1.call-start = ((), (), s32[]{:S(2)}) async-start(), calls=%async_computation.3 | async-start | bytes 28835840 | tf_op jit(solution)/shard_map/all_gather | solution.py:52
  27.3 0.6 copy-start.5
  144.6 236.5 %all-to-all-start = ((bf16[32,320,1024]{2,1,0:T(8,128)(2,1)}), bf16[32,320,1024]{2,1,0:T(8,128)(2,1)}, u32[]{:S(2)}, u32[]{:S(2)}) async-start(bf16[32,320,1024]{2,1,0:T(8,128)(2,1)} %broadcast_select_fusion.1), calls=%async_computation | async-start | bytes 41943040 | tf_op jit(solution)/shard_map/all_to_all | solution.py:54
  152.6 479.1 %all-gather.8.cloned.1.call-start = ((), (), s32[]{:S(2)}) async-start(), calls=%async_computation.4 | async-start | bytes 28835840 | tf_op jit(solution)/shard_map/all_gather | solution.py:53
  728.6 8.6 copy-start.6
  728.6 11.3 copy-start.3
  728.6 236.9 %all-to-all-start.1 = ((bf16[4,2560,1024]{2,0,1:T(4,128)(2,1)}), bf16[4,2560,1024]{2,0,1:T(4,128)(2,1)}, u32[]{:S(2)}, u32[]{:S(2)}) async-start(bf16[4,2560,1024]{2,0,1:T(4,128)(2,1)} %copy.42), calls=%async_computation.1 | async-start | bytes 41943040 | tf_op jit(solution)/shard_map/all_to_all | solution.py:56
  750.9 68.3 %copy-start.4 = (s32[4096,2]{0,1:T(2,128)S(1)}, s32[4096,2]{0,1:T(2,128)}, u32[]{:S(2)}) copy-start(s32[4096,2]{0,1:T(2,128)} %param.13) | copy-start | bytes 98308
  750.9 69.1 %copy-start.8 = (pred[4096,2]{0,1:T(4,128)(4,1)S(1)}, pred[4096,2]{0,1:T(4,128)(4,1)}, u32[]{:S(2)}) copy-start(pred[4096,2]{0,1:T(4,128)(4,1)} %get-tuple-element.7) | copy-start | bytes 24580
  750.9 70.0 %copy-start.7 = (s32[8192]{0:T(1024)S(1)}, s32[8192]{0:T(1024)}, u32[]{:S(2)}) copy-start(s32[8192]{0:T(1024)} %reshape.132) | copy-start | bytes 98308
  1061.9 90.3 %copy-start.1 = (bf16[1024,32]{0,1:T(8,128)(2,1)S(1)}, bf16[1024,32]{0,1:T(8,128)(2,1)}, u32[]{:S(2)}) copy-start(bf16[1024,32]{0,1:T(8,128)(2,1)} %param.9) | copy-start | bytes 196612
Sparse Core Ops, SparseCore 0:
  8.9 207.2 all-gather.3
  217.8 204.4 all-gather.5
  423.9 207.7 all-gather.7
where the time goes:
time: 1170 us; the launch traced here: 1160 us
  waiting for transfers between devices  447 us (38%)
  local copies, waits for them, and re-layouts  313 us (27%)
  matrix products  236 us (20%)
  other arithmetic  133 us (11%)
  starting transfers between devices  16.7 us (1%)
  between operations  13.9 us (1%)
    all_to_all x1, waiting for transfers between devices, local_block(): recv_rows = lax.all_to_all(send_rows, 'ep', 0, 1, tiled=True)  228 us
    all_to_all x1, waiting for transfers between devices, local_block(): back_rows = lax.all_to_all(expert_out, 'ep', 1, 0, tiled=True)  145 us
    dot_general x1, matrix products, expert_block(): jnp.einsum('ecd,edf->ecf', rows_in, up_full, preferred_element_type=jnp.f...  86.3 us
    reduce_sum x1, other arithmetic, local_block(): jnp.sum(gate_probs[:, :, None] * returned.astype(jnp.float32), axis=1)  78.3 us
    gather x2, local copies, waits for them, and re-layouts, take_slots(): return jnp.take(expert_rows, slot_ids, axis=0, mode='fill', fill_value=0)  75.2 us
    dot_general x1, matrix products, expert_block(): jnp.einsum('ecd,edf->ecf', rows_in, gate_full, preferred_element_type=jnp...  74.1 us
    all_gather x1, waiting for transfers between devices, local_block(): down_full = lax.all_gather(w_down, 'fsdp', axis=2, tiled=True)  72.8 us
    gather x5, local copies, waits for them, and re-layouts, norm_and_gates(): jnp.take_along_axis(logits, top2_ids, axis=1)  70.1 us
  transfers between devices with their start and end apart: 5, of which 3 were waited for; matrix products, arithmetic and copies ran while one was open for 34% of the time, Pallas kernels for 0%

commit v1 on v0

v1 whole, which is shorter than its diff:
```python
import functools
from typing import NamedTuple

import jax
import jax.numpy as jnp
from jax import lax
from jax.experimental import pallas as pl
from jax.experimental.pallas import tpu as pltpu
from jax.sharding import PartitionSpec as P

EPS = 1e-5
TILE = 256
WIN = 64
ALIGN = 16
VMEM_LIMIT = 60 * 1024 * 1024


def norm_and_gates(hidden, norm_gain, w_router, top2_ids):
    hidden_f32 = hidden.astype(jnp.float32)
    mean_sq = jnp.mean(hidden_f32 * hidden_f32, axis=-1, keepdims=True)
    normed = (hidden_f32 * lax.rsqrt(mean_sq + EPS) * norm_gain.astype(jnp.float32)).astype(jnp.bfloat16)
    logits = jnp.dot(normed, w_router, preferred_element_type=jnp.float32)
    experts = jnp.arange(w_router.shape[1], dtype=jnp.int32)[None, :]
    picked = [jnp.sum(jnp.where(top2_ids[:, k:k + 1] == experts, logits, 0.0), axis=1) for k in range(2)]
    gate_probs = jax.nn.softmax(jnp.stack(picked, axis=1), axis=-1)
    return normed, gate_probs


def route(top2_ids, num_experts, capacity):
    tok_count = top2_ids.shape[0]
    experts = jnp.arange(num_experts, dtype=jnp.int32)[None, :]
    hit0 = top2_ids[:, 0:1] == experts
    hit1 = top2_ids[:, 1:2] == experts
    chosen = (hit0 | hit1).astype(jnp.bfloat16)
    block = 128
    blocks = chosen.reshape(tok_count // block, block, num_experts)
    strict = (jnp.arange(block)[:, None] > jnp.arange(block)[None, :]).astype(jnp.bfloat16)
    inside = jnp.einsum('st,bte->bse', strict, blocks, preferred_element_type=jnp.float32)
    totals = jnp.sum(blocks.astype(jnp.float32), axis=1)
    count = tok_count // block
    before = jnp.sum(jnp.where((jnp.arange(count)[:, None] > jnp.arange(count)[None, :])[:, :, None], totals[None], 0.0), axis=1)
    rank = (inside + before[:, None, :]).reshape(tok_count, num_experts).astype(jnp.int32)
    slots = []
    for k, hit in enumerate((hit0, hit1)):
        pos = jnp.sum(jnp.where(hit, rank, 0), axis=1)
        slots.append(jnp.where(pos < capacity, top2_ids[:, k] * capacity + pos, -1))
    kept = (hit0 | hit1) & (rank < capacity)
    per_expert = jnp.where(kept, rank, -1).T
    step = TILE // block
    starts = jnp.concatenate([before[::step], (before[-1:] + totals[-1:])], axis=0)
    starts = jnp.minimum(starts.astype(jnp.int32), capacity)
    return slots, per_expert, starts


def window(starts_ref, tile, expert, round_idx, capacity):
    first = starts_ref[tile, expert] // ALIGN * ALIGN + round_idx * WIN
    base = jnp.minimum(first, capacity - WIN)
    return pl.multiple_of(base, ALIGN), first


def round_count(starts_ref, tile, experts, capacity):
    need = jnp.int32(0)
    for expert in experts:
        low = starts_ref[tile, expert] // ALIGN * ALIGN
        need = jnp.maximum(need, starts_ref[tile + 1, expert] - low)
    return (need + WIN - 1) // WIN


def combine_kernel(experts, local, capacity, count, starts_ref, tok_ref, acc_ref, *refs):
    rets, out_ref, stage, total = refs[:count], refs[count], refs[count + 1], refs[count + 2]
    tile = pl.program_id(0)
    total[...] = acc_ref[...].astype(jnp.float32)
    width = 8 * WIN
    lane = lax.broadcasted_iota(jnp.int32, (1, width), 1)
    which = lane // WIN
    inner = lane % WIN

    def one_round(round_idx, carry):
        for g in range(0, len(experts), 8):
            slot = jnp.zeros((1, width), jnp.int32)
            valid = jnp.zeros((1, width), jnp.int32)
            for i, e in enumerate(experts[g:g + 8]):
                base, first = window(starts_ref, tile, e, round_idx, capacity)
                stage[i * WIN:(i + 1) * WIN, :] = rets[0][e % local, e // local, pl.ds(base, WIN), :]
                slot = jnp.where(which == i, e * capacity + base, slot)
                valid = jnp.where(which == i, e * capacity + first, valid)
            slot = slot + inner
            slot = jnp.where(slot >= valid, slot, -2).astype(jnp.float32)
            for k in range(2):
                pick = jnp.where(tok_ref[:, k:k + 1] == slot, 1.0, 0.0).astype(jnp.bfloat16)
                got = jnp.dot(pick, stage[...], preferred_element_type=jnp.float32)
                total[...] += tok_ref[:, 2 + k:3 + k] * got
        return carry

    lax.fori_loop(0, round_count(starts_ref, tile, experts, capacity), one_round, 0)
    out_ref[...] = total[...].astype(out_ref.dtype)


def combine(acc, rets, indices, tok, starts, num_experts, capacity, local, out_dtype):
    tok_count, d_model = acc.shape
    dests = num_experts // local
    experts = [j * local + i for i in indices for j in range(dests)]
    shape = rets[0].shape
    return pl.pallas_call(
        functools.partial(combine_kernel, experts, local, capacity, len(rets)),
        out_shape=jax.ShapeDtypeStruct(acc.shape, out_dtype),
        grid_spec=pltpu.PrefetchScalarGridSpec(
            num_scalar_prefetch=1,
            grid=(tok_count // TILE,),
            in_specs=[
                pl.BlockSpec((TILE, 4), lambda t, s: (t, 0)),
                pl.BlockSpec((TILE, d_model), lambda t, s: (t, 0)),
            ] + [pl.BlockSpec(shape, lambda t, s: (0, 0, 0, 0), pipeline_mode=pl.Buffered(1))] * len(rets),
            out_specs=pl.BlockSpec((TILE, d_model), lambda t, s: (t, 0)),
            scratch_shapes=[pltpu.VMEM((8 * WIN, d_model), jnp.bfloat16), pltpu.VMEM((TILE, d_model), jnp.float32)],
        ),
        compiler_params=pltpu.CompilerParams(dimension_semantics=('arbitrary',), vmem_limit_bytes=VMEM_LIMIT),
        cost_estimate=pl.CostEstimate(flops=4 * tok_count * len(experts) * WIN * d_model, bytes_accessed=8 * tok_count * d_model, transcendentals=0),
        name='combine_rows',
    )(starts, tok, acc, *rets)


class Unit(NamedTuple):
    expert: int
    kind: int
    low: int
    size: int


GATE, UP, DOWN = 0, 1, 2
MESH = pl.DeviceIdType.MESH
AHEAD = 3
FFB = 256


def unit_list(local, ff):
    units = []
    cuts = [0, 1024, 2048, ff]
    for e in range(local):
        if e < local - 1:
            units += [Unit(e, GATE, 0, ff), Unit(e, UP, 0, ff)]
        else:
            for low, high in zip(cuts[:-1], cuts[1:]):
                units += [Unit(e, GATE, low, high - low), Unit(e, UP, low, high - low)]
        units.append(Unit(e, DOWN, 0, ff))
    return units


def moe_kernel(units, capacity, slots_ref, normed_hbm, gate_hbm, up_hbm, down_hbm,
               ret_hbm, send_hbm, recv_hbm, out_hbm, gate_all, up_all, down_all,
               normed, stage, rows, act, wbuf, dbuf, obuf,
               w_send, w_recv, a_send, a_recv, r_send, r_recv, c_send, c_recv,
               normed_sem, stage_sem, rows_sem, wbuf_sem, dbuf_sem, obuf_sem):
    local, d_shard, ff = gate_hbm.shape
    fsdp = gate_all.shape[1]
    dests = recv_hbm.shape[1]
    f_me, j_me = lax.axis_index('fsdp'), lax.axis_index('ep')
    right, left, far = lax.rem(f_me + 1, fsdp), lax.rem(f_me + fsdp - 1, fsdp), lax.rem(f_me + 2, fsdp)
    last = local - 1
    index = {(u.expert, u.kind, u.low): c for c, u in enumerate(units)}

    barrier = pltpu.get_barrier_semaphore()
    pl.semaphore_signal(barrier, inc=1, device_id={'fsdp': right}, device_id_type=MESH)
    pl.semaphore_signal(barrier, inc=1, device_id={'fsdp': left}, device_id_type=MESH)
    for step in range(1, dests):
        pl.semaphore_signal(barrier, inc=1, device_id={'ep': lax.rem(j_me + step, dests)}, device_id_type=MESH)
    pl.semaphore_wait(barrier, 2 + dests - 1)

    def own_part(u):
        if u.kind == DOWN:
            return down_hbm.at[u.expert]
        return (gate_hbm, up_hbm)[u.kind].at[u.expert, :, pl.ds(u.low, u.size)]

    def all_part(u, f, half=None):
        if u.kind == DOWN:
            span = pl.ds(0, ff) if half is None else pl.ds(half * (ff // 2), ff // 2)
            return down_all.at[u.expert, f, span, :]
        span = pl.ds(0, d_shard) if half is None else pl.ds(half * (d_shard // 2), d_shard // 2)
        return (gate_all, up_all)[u.kind].at[u.expert, f, span, pl.ds(u.low, u.size)]

    def direct(c, way):
        u = units[c]
        return pltpu.make_async_remote_copy(
            src_ref=own_part(u), dst_ref=all_part(u, f_me), send_sem=w_send.at[c, way], recv_sem=w_recv.at[c, way],
            device_id={'fsdp': (right, left)[way]}, device_id_type=MESH)

    def forward(c, way):
        u = units[c]
        part = all_part(u, (left, right)[way], way)
        return pltpu.make_async_remote_copy(
            src_ref=part, dst_ref=part, send_sem=w_send.at[c, 2 + way], recv_sem=w_recv.at[c, 2 + way],
            device_id={'fsdp': (right, left)[way]}, device_id_type=MESH)

    def start_direct(c):
        for way in range(2):
            direct(c, way).start()

    def service(c, then):
        for way in range(2):
            direct(c, way).wait_recv()
            forward(c, way).start()
        for n in then:
            start_direct(n)

    def wait_far(c):
        for way in range(2):
            forward(c, way).wait_recv()

    for c in range(AHEAD):
        start_direct(c)
    load = pltpu.make_async_copy(normed_hbm, normed, normed_sem)
    load.start()
    load.wait()

    def dest_of(step):
        return lax.rem(j_me + 1 + step, dests)

    def store_rows(i, step):
        slot = lax.rem(step, 2)
        return pltpu.make_async_copy(stage.at[slot], send_hbm.at[i, dest_of(step)], stage_sem.at[slot])

    def send_rows(i, step):
        j = dest_of(step)
        return pltpu.make_async_remote_copy(
            src_ref=send_hbm.at[i, j], dst_ref=recv_hbm.at[i, j_me], send_sem=a_send.at[i, step], recv_sem=a_recv.at[i, j_me],
            device_id={'ep': j}, device_id_type=MESH)

    row_iota = lax.broadcasted_iota(jnp.int32, (capacity, normed.shape[0]), 0)

    def dispatch(i):
        def body(step, carry):
            want = slots_ref[pl.ds(dest_of(step) * local + i, 1), :]
            pick = jnp.where(row_iota == want, 1.0, 0.0).astype(jnp.bfloat16)
            stage[lax.rem(step, 2)] = jnp.dot(pick, normed[...], preferred_element_type=jnp.float32).astype(jnp.bfloat16)

            @pl.when(step > 0)
            def _():
                store_rows(i, step - 1).wait()
                send_rows(i, step - 1).start()

            store_rows(i, step).start()
            return carry

        lax.fori_loop(0, dests, body, 0)
        store_rows(i, dests - 1).wait()

    def load_rows(e):
        def copy(step):
            j = dest_of(step)
            if step == dests - 1:
                return pltpu.make_async_copy(send_hbm.at[e, j], rows.at[j], rows_sem.at[step])
            return pltpu.make_async_copy(recv_hbm.at[e, j], rows.at[j], rows_sem.at[step])

        for step in range(dests - 1):
            j = dest_of(step)
            pltpu.make_async_remote_copy(
                src_ref=send_hbm.at[e, j], dst_ref=recv_hbm.at[e, j], send_sem=a_send.at[e, step], recv_sem=a_recv.at[e, j],
                device_id={'ep': j}, device_id_type=MESH).wait_recv()
        for step in range(dests):
            copy(step).start()
        for step in range(dests):
            copy(step).wait()

    def block_copies(e, b, slot):
        cols = pl.ds(pl.multiple_of(b * FFB, FFB), FFB)
        copies = []
        for m, (own, whole) in enumerate(((gate_hbm, gate_all), (up_hbm, up_all))):
            for r in range(fsdp):
                f = lax.rem(f_me + r, fsdp)
                src = own.at[e, :, cols] if r == 0 else whole.at[e, f, :, cols]
                copies.append(pltpu.make_async_copy(src, wbuf.at[slot, m, f], wbuf_sem.at[slot, m, r]))
        return copies

    def phase_one(e, low, high):
        for copy in block_copies(e, low, low % 2):
            copy.start()

        def body(b, carry):
            slot = lax.rem(b, 2)

            @pl.when(b + 1 < high)
            def _():
                for copy in block_copies(e, b + 1, 1 - slot):
                    copy.start()

            for copy in block_copies(e, b, slot):
                copy.wait()
            gate = wbuf[slot, GATE].reshape(fsdp * d_shard, FFB)
            up = wbuf[slot, UP].reshape(fsdp * d_shard, FFB)
            for r in range(dests // 2):
                x = rows[2 * r:2 * r + 2].reshape(2 * capacity, fsdp * d_shard)
                a = jnp.dot(x, gate, preferred_element_type=jnp.float32)
                u = jnp.dot(x, up, preferred_element_type=jnp.float32)
                act[2 * r * capacity:(2 * r + 2) * capacity, pl.ds(pl.multiple_of(b * FFB, FFB), FFB)] = (a * jax.nn.sigmoid(a) * u).astype(jnp.bfloat16)
            return carry

        lax.fori_loop(low, high, body, 0)

    def back_rows(e, step):
        j = dest_of(step)
        return pltpu.make_async_remote_copy(
            src_ref=out_hbm.at[e, j], dst_ref=ret_hbm.at[e, j_me], send_sem=r_send.at[e, step], recv_sem=r_recv.at[e, j_me],
            device_id={'ep': j}, device_id_type=MESH)

    def back_cols(n, f, step):
        j = dest_of(step)
        cols = pl.ds(pl.multiple_of(f * d_shard, d_shard), d_shard)
        return pltpu.make_async_remote_copy(
            src_ref=out_hbm.at[last, j, :, cols], dst_ref=ret_hbm.at[last, j_me, :, cols], send_sem=c_send.at[n, step], recv_sem=c_recv.at[f, j_me],
            device_id={'ep': j}, device_id_type=MESH)

    order = (f_me, left, right, far)

    def down_load(e, n):
        src = down_hbm.at[e] if n == 0 else down_all.at[e, order[n]]
        return pltpu.make_async_copy(src, dbuf.at[n % 2], dbuf_sem.at[n % 2])

    def down_column(e, n):
        f = order[n]

        def body(r, carry):
            hid = act[pl.ds(pl.multiple_of(r * 2 * capacity, 2 * capacity), 2 * capacity), :]
            got = jnp.dot(hid, dbuf[n % 2], preferred_element_type=jnp.float32).astype(jnp.bfloat16)
            obuf[pl.ds(2 * r, 2)] = got.reshape(2, capacity, d_shard)
            return carry

        lax.fori_loop(0, dests // 2, body, 0)
        cols = pl.ds(pl.multiple_of(f * d_shard, d_shard), d_shard)
        mine = pltpu.make_async_copy(obuf.at[j_me], ret_hbm.at[e, j_me, :, cols], obuf_sem.at[0])
        rest = pltpu.make_async_copy(obuf, out_hbm.at[e, :, :, cols], obuf_sem.at[1])
        mine.start()
        rest.start()
        mine.wait()
        rest.wait()

    def phase_two(e, far_unit):
        down_load(e, 0).start()
        down_load(e, 1).start()
        down_load(e, 0).wait()
        down_column(e, 0)
        if e == last:
            for step in range(dests - 1):
                back_cols(0, order[0], step).start()
        down_load(e, 2).start()
        down_load(e, 1).wait()
        down_column(e, 1)
        if e == last:
            for step in range(dests - 1):
                back_cols(1, order[1], step).start()
        down_load(e, 2).wait()
        down_column(e, 2)
        if e == last:
            for step in range(dests - 1):
                back_cols(2, order[2], step).start()
        wait_far(far_unit)
        down_load(e, 3).start()
        down_load(e, 3).wait()
        down_column(e, 3)
        for step in range(dests - 1):
            if e == last:
                back_cols(3, order[3], step).start()
            else:
                back_rows(e, step).start()

    first_last = index[last, GATE, 0]
    final = index[last, DOWN, 0]

    def then(c):
        n = c + AHEAD
        if n < final:
            return (n,)
        return (final,) if c == final - 1 else ()

    done = 0

    def serve(upto):
        nonlocal done
        while done <= upto:
            service(done, then(done))
            done += 1

    for i in range(local):
        dispatch(i)
        if i < local - 1:
            serve(i)
    blocks = ff // FFB
    for e in range(last):
        g = index[e, GATE, 0]
        serve(g + 3)
        wait_far(g)
        wait_far(g + 1)
        load_rows(e)
        phase_one(e, 0, blocks)
        serve(g + 4 if e < last - 1 else g + 5)
        phase_two(e, g + 2)
        serve(g + 5 if e < last - 1 else g + 6)
    load_rows(last)
    for c in range(first_last, final, 2):
        serve(min(c + 5, final - 1))
        wait_far(c)
        wait_far(c + 1)
        low = units[c].low // FFB
        phase_one(last, low, low + units[c].size // FFB)
    serve(final)
    phase_two(last, final)

    for e in range(last):
        for step in range(dests - 1):
            j = dest_of(step)
            pltpu.make_async_remote_copy(
                src_ref=out_hbm.at[e, j], dst_ref=ret_hbm.at[e, j], send_sem=r_send.at[e, step], recv_sem=r_recv.at[e, j],
                device_id={'ep': j}, device_id_type=MESH).wait_recv()
    for n in range(fsdp):
        cols = pl.ds(n * d_shard, d_shard)
        for step in range(dests - 1):
            j = dest_of(step)
            pltpu.make_async_remote_copy(
                src_ref=out_hbm.at[last, j, :, cols], dst_ref=ret_hbm.at[last, j, :, cols], send_sem=c_send.at[n, step], recv_sem=c_recv.at[n, j],
                device_id={'ep': j}, device_id_type=MESH).wait_recv()
    for c in range(len(units)):
        for way in range(2):
            direct(c, way).wait_send()
            forward(c, way).wait_send()
    for step in range(dests - 1):
        for i in range(local):
            send_rows(i, step).wait_send()
        for e in range(last):
            back_rows(e, step).wait_send()
        for n in range(fsdp):
            back_cols(n, order[n], step).wait_send()


def exchange(per_expert, normed, w_gate, w_up, w_down, fsdp, dests, capacity):
    local, d_shard, ff = w_gate.shape
    tok_count, d_model = normed.shape
    units = unit_list(local, ff)
    rows = (local, dests, capacity, d_model)
    bf16 = jnp.bfloat16
    shapes = [rows, rows, rows, rows, (local, fsdp, d_shard, ff), (local, fsdp, d_shard, ff), (local, fsdp, ff, d_shard)]
    dma = pltpu.SemaphoreType.DMA
    anywhere = pl.BlockSpec(memory_space=pl.ANY)
    return pl.pallas_call(
        functools.partial(moe_kernel, units, capacity),
        out_shape=[jax.ShapeDtypeStruct(s, bf16) for s in shapes],
        in_specs=[pl.BlockSpec(memory_space=pltpu.VMEM)] + [anywhere] * 4,
        out_specs=[anywhere] * len(shapes),
        scratch_shapes=[
            pltpu.VMEM((tok_count, d_model), bf16),
            pltpu.VMEM((2, capacity, d_model), bf16),
            pltpu.VMEM((dests, capacity, d_model), bf16),
            pltpu.VMEM((dests * capacity, ff), bf16),
            pltpu.VMEM((2, 2, fsdp, d_shard, FFB), bf16),
            pltpu.VMEM((2, ff, d_shard), bf16),
            pltpu.VMEM((dests, capacity, d_shard), bf16),
            dma((len(units), 4)), dma((len(units), 4)),
            dma((local, dests)), dma((local, dests)),
            dma((local, dests)), dma((local, dests)),
            dma((fsdp, dests)), dma((fsdp, dests)),
            dma, dma((2,)), dma((dests,)), dma((2, 2, fsdp)), dma((2,)), dma((2,)),
        ],
        compiler_params=pltpu.CompilerParams(collective_id=0, has_side_effects=True, vmem_limit_bytes=VMEM_LIMIT),
        name='moe_exchange',
    )(per_expert, normed, w_gate, w_up, w_down)[0]


def local_block(hidden, norm_gain, w_router, w_gate, w_up, w_down, top2_ids, *, fsdp, dests):
    tok_local, d_model = hidden.shape
    num_experts = w_router.shape[1]
    local = w_gate.shape[0]
    capacity = (5 * tok_local + 2 * num_experts - 1) // (2 * num_experts)
    normed, gate_probs = norm_and_gates(hidden, norm_gain, w_router, top2_ids)
    slots, per_expert, starts = route(top2_ids, num_experts, capacity)
    tok = jnp.stack([slots[0].astype(jnp.float32), slots[1].astype(jnp.float32), gate_probs[:, 0], gate_probs[:, 1]], axis=1)
    ret = exchange(per_expert, normed, w_gate, w_up, w_down, fsdp, dests, capacity)
    return combine(hidden, [ret], list(range(local)), tok, starts, num_experts, capacity, local, jnp.bfloat16)


def solution(mesh):
    tok_spec = P(('dp', 'fsdp', 'ep'), None)
    in_specs = (tok_spec, P(None), P(None, None), P('ep', 'fsdp', None), P('ep', 'fsdp', None), P('ep', None, 'fsdp'), tok_spec)
    block = functools.partial(local_block, fsdp=mesh.shape['fsdp'], dests=mesh.shape['ep'])
    return jax.shard_map(block, mesh=mesh, in_specs=in_specs, out_specs=tok_spec, check_vma=False)
```

time: 1170 us -> 701 us (0.60)
  Pallas kernels: 0 us -> 674 us
  waiting for transfers between devices: 447 us -> 0 us
  local copies, waits for them, and re-layouts: 313 us -> 6.23 us
  matrix products: 236 us -> 3.08 us
  other arithmetic: 133 us -> 14.1 us
  starting transfers between devices: 16.7 us -> 0 us
  between operations: 13.9 us -> 0.31 us
    pallas_call x0 -> x2, Pallas kernels: none -> 674 us  [the longest x1 620 us: exchange(): pl.pallas_call(functools.partial(moe_kernel, units, capacity), out_shape=...]
    all_to_all x2 -> x0, waiting for transfers between devices: 372 us -> none  [the longest x1 228 us: local_block(): recv_rows = lax.all_to_all(send_rows, 'ep', 0, 1, tiled=True)]
    dot_general x3 -> x1, matrix products: 230 us -> 0.41 us  [route(): jnp.einsum('st,bte->bse', strict, blocks, preferred_element_type=jnp.floa...]
    gather x8 -> x0, local copies, waits for them, and re-layouts: 200 us -> none  [the longest x2 75.2 us: take_slots(): return jnp.take(expert_rows, slot_ids, axis=0, mode='fill', fill_value=0)]
    reduce_sum x3, other arithmetic: 79.1 us -> 0.55 us  [the longest x1 0.25 us: route(): totals = jnp.sum(blocks.astype(jnp.float32), axis=1)]
    all_gather x3 -> x0, waiting for transfers between devices: 72.8 us -> none  [the longest x1 72.8 us: local_block(): down_full = lax.all_gather(w_down, 'fsdp', axis=2, tiled=True)]
    all_to_all x2 -> x0, local copies, waits for them, and re-layouts: 38.8 us -> none  [the longest x1 21.2 us: local_block(): back_rows = lax.all_to_all(expert_out, 'ep', 1, 0, tiled=True)]
    scatter x1 -> x0, local copies, waits for them, and re-layouts: 30.9 us -> none  [gather_rows(): jnp.full((num_slots,), tok_count, dtype=jnp.int32).at[slot_ids.reshape(-1)]]
  transfers between devices with their start and end apart: 5 -> 0, of which waited for: 3 -> 0; matrix products, arithmetic and copies ran while one was open for 34% -> 0% of each run, Pallas kernels for 0% -> 0%
where the time goes in v1:
time: 701 us; the launch traced here: 698 us
  Pallas kernels  674 us (96%)
  other arithmetic  14.1 us (2%)
    pallas_call x1, Pallas kernels, exchange(): pl.pallas_call(functools.partial(moe_kernel, units, capacity), out_shape=...  620 us
    pallas_call x1, Pallas kernels, combine(): pl.pallas_call(functools.partial(combine_kernel, experts, local, capacity...  53.7 us

profile of v1, /device:TPU:97, one launch (start us, length us, event | category | flops | bytes accessed | tf_op | source)
XLA Modules:
  0.0 697.6 jit_solution(7117635612000066477)
XLA Ops:
  0.0 0.0 copy-start
  0.0 0.7 convert_element_type.48
  0.7 5.1 fusion
  5.8 0.9 fusion.21
  6.7 0.3 convert_reduce_fusion
  7.0 0.2 select_reduce_fusion.2
  7.2 0.6 fusion.19.starts_ref
  7.8 0.4 fusion.5
  8.2 0.9 fusion.17
  9.1 0.9 fusion.4.slots_ref
  10.0 5.2 fusion.2.normed_hbm
  15.3 0.0 copy-start.2
  15.3 3.4 copy-done.2
  18.7 0.0 copy-done
  18.7 2.7 select_reduce_fusion
  21.4 0.1 fusion.20
  21.4 0.1 broadcast_divide_fusion
  21.5 0.1 pad_maximum_fusion
  21.6 1.9 copy.23.tok_ref
  23.5 620.2 %moe_exchange.1 = (bf16[4,8,320,1024]{3,2,1,0:T(8,128)(2,1)}, bf16[4,8,320,1024]{3,2,1,0:T(8,128)(2,1)}, bf16[4,8,320,1024]{3,2,1,0:T(8,128)(2,1)}, bf16[4,8,320...) custom-call(s32[32,4096]{1,0:T(8,128)} %fusion.4.slots_ref, ...), custom_call_target="tpu_custom_call" | custom-call | tf_op jit(solution)/shard_map/moe_exchange/pallas_call | solution.py:442
  643.7 0.0 copy-start.1
  643.7 53.7 %combine_rows.1 = bf16[4096,1024]{1,0:T(8,128)(2,1)} custom-call(s32[17,32]{1,0:T(8,128)} %fusion.19.starts_ref, f32[4096,4]{1,0:T(8,128)} %copy.23.tok_ref, bf16[4096,1024]{1,0:T(8,128)(2,1)} %acc_ref.1, bf16[4,8,320,1024]{3,2,1,0:T(8,128)(2,1)} %get-tuple-element.6.refs_0_), custom_call_target="tpu_custom_call" | custom-call | flops 34359738368 | bytes 33554432 | tf_op jit(solution)/shard_map/combine_rows/pallas_call | solution.py:104
  697.4 0.0 copy-done.1
  (5 shorter events, 0.0 us)
Async XLA Ops:
  0.0 18.7 %copy-start = (bf16[1024,32]{0,1:T(8,128)(2,1)S(1)}, bf16[1024,32]{0,1:T(8,128)(2,1)}, u32[]{:S(2)}) copy-start(bf16[1024,32]{0,1:T(8,128)(2,1)} %param.9) | copy-start | bytes 196612
  15.3 3.4 copy-start.2
  643.7 53.7 %copy-start.1 = (bf16[1024,32]{0,1:T(8,128)(2,1)S(1)}, bf16[1024,32]{0,1:T(8,128)(2,1)}, u32[]{:S(2)}) copy-start(bf16[1024,32]{0,1:T(8,128)(2,1)} %param.9) | copy-start | bytes 196612

commit v2 on v1

--- a/solution.py
+++ b/solution.py
@@ -9,51 +9,16 @@
 from jax.sharding import PartitionSpec as P
 
 EPS = 1e-5
-TILE = 256
-WIN = 64
-ALIGN = 16
+TILE = 128
+WIN = 32
+SUB = 1
+ALIGN = 8
+ROUTE = 512
 VMEM_LIMIT = 60 * 1024 * 1024
 
 
-def norm_and_gates(hidden, norm_gain, w_router, top2_ids):
-    hidden_f32 = hidden.astype(jnp.float32)
-    mean_sq = jnp.mean(hidden_f32 * hidden_f32, axis=-1, keepdims=True)
-    normed = (hidden_f32 * lax.rsqrt(mean_sq + EPS) * norm_gain.astype(jnp.float32)).astype(jnp.bfloat16)
-    logits = jnp.dot(normed, w_router, preferred_element_type=jnp.float32)
-    experts = jnp.arange(w_router.shape[1], dtype=jnp.int32)[None, :]
-    picked = [jnp.sum(jnp.where(top2_ids[:, k:k + 1] == experts, logits, 0.0), axis=1) for k in range(2)]
-    gate_probs = jax.nn.softmax(jnp.stack(picked, axis=1), axis=-1)
-    return normed, gate_probs
-
-
-def route(top2_ids, num_experts, capacity):
-    tok_count = top2_ids.shape[0]
-    experts = jnp.arange(num_experts, dtype=jnp.int32)[None, :]
-    hit0 = top2_ids[:, 0:1] == experts
-    hit1 = top2_ids[:, 1:2] == experts
-    chosen = (hit0 | hit1).astype(jnp.bfloat16)
-    block = 128
-    blocks = chosen.reshape(tok_count // block, block, num_experts)
-    strict = (jnp.arange(block)[:, None] > jnp.arange(block)[None, :]).astype(jnp.bfloat16)
-    inside = jnp.einsum('st,bte->bse', strict, blocks, preferred_element_type=jnp.float32)
-    totals = jnp.sum(blocks.astype(jnp.float32), axis=1)
-    count = tok_count // block
-    before = jnp.sum(jnp.where((jnp.arange(count)[:, None] > jnp.arange(count)[None, :])[:, :, None], totals[None], 0.0), axis=1)
-    rank = (inside + before[:, None, :]).reshape(tok_count, num_experts).astype(jnp.int32)
-    slots = []
-    for k, hit in enumerate((hit0, hit1)):
-        pos = jnp.sum(jnp.where(hit, rank, 0), axis=1)
-        slots.append(jnp.where(pos < capacity, top2_ids[:, k] * capacity + pos, -1))
-    kept = (hit0 | hit1) & (rank < capacity)
-    per_expert = jnp.where(kept, rank, -1).T
-    step = TILE // block
-    starts = jnp.concatenate([before[::step], (before[-1:] + totals[-1:])], axis=0)
-    starts = jnp.minimum(starts.astype(jnp.int32), capacity)
-    return slots, per_expert, starts
-
-
 def window(starts_ref, tile, expert, round_idx, capacity):
-    first = starts_ref[tile, expert] // ALIGN * ALIGN + round_idx * WIN
+    first = starts_ref[expert, tile] // ALIGN * ALIGN + round_idx * WIN
     base = jnp.minimum(first, capacity - WIN)
     return pl.multiple_of(base, ALIGN), first
 
@@ -61,63 +26,77 @@
 def round_count(starts_ref, tile, experts, capacity):
     need = jnp.int32(0)
     for expert in experts:
-        low = starts_ref[tile, expert] // ALIGN * ALIGN
-        need = jnp.maximum(need, starts_ref[tile + 1, expert] - low)
+        low = starts_ref[expert, tile] // ALIGN * ALIGN
+        need = jnp.maximum(need, starts_ref[expert, tile + 1] - low)
     return (need + WIN - 1) // WIN
 
 
-def combine_kernel(experts, local, capacity, count, starts_ref, tok_ref, acc_ref, *refs):
-    rets, out_ref, stage, total = refs[:count], refs[count], refs[count + 1], refs[count + 2]
-    tile = pl.program_id(0)
-    total[...] = acc_ref[...].astype(jnp.float32)
-    width = 8 * WIN
-    lane = lax.broadcasted_iota(jnp.int32, (1, width), 1)
-    which = lane // WIN
-    inner = lane % WIN
-
-    def one_round(round_idx, carry):
-        for g in range(0, len(experts), 8):
-            slot = jnp.zeros((1, width), jnp.int32)
-            valid = jnp.zeros((1, width), jnp.int32)
-            for i, e in enumerate(experts[g:g + 8]):
-                base, first = window(starts_ref, tile, e, round_idx, capacity)
-                stage[i * WIN:(i + 1) * WIN, :] = rets[0][e % local, e // local, pl.ds(base, WIN), :]
-                slot = jnp.where(which == i, e * capacity + base, slot)
-                valid = jnp.where(which == i, e * capacity + first, valid)
-            slot = slot + inner
-            slot = jnp.where(slot >= valid, slot, -2).astype(jnp.float32)
-            for k in range(2):
-                pick = jnp.where(tok_ref[:, k:k + 1] == slot, 1.0, 0.0).astype(jnp.bfloat16)
-                got = jnp.dot(pick, stage[...], preferred_element_type=jnp.float32)
-                total[...] += tok_ref[:, 2 + k:3 + k] * got
-        return carry
-
-    lax.fori_loop(0, round_count(starts_ref, tile, experts, capacity), one_round, 0)
-    out_ref[...] = total[...].astype(out_ref.dtype)
-
-
-def combine(acc, rets, indices, tok, starts, num_experts, capacity, local, out_dtype):
-    tok_count, d_model = acc.shape
-    dests = num_experts // local
-    experts = [j * local + i for i in indices for j in range(dests)]
-    shape = rets[0].shape
+def combine_kernel(local, capacity, starts_ref, tok_ref, hidden_ref, ret_ref, out_ref, total):
+    dests = ret_ref.shape[1]
+    experts = [j * local + i for i in range(local) for j in range(dests)]
+    width, lanes = len(experts) * WIN, 128
+    spot = lax.broadcasted_iota(jnp.int32, (width // lanes, lanes), 0) * lanes + lax.broadcasted_iota(jnp.int32, (width // lanes, lanes), 1)
+    which, inner = spot // WIN, spot % WIN
+
+    def gathered(tile, tok, round_idx):
+        slot = jnp.zeros(spot.shape, jnp.int32)
+        valid = jnp.zeros(spot.shape, jnp.int32)
+        rows = []
+        for n, e in enumerate(experts):
+            base, first = window(starts_ref, tile, e, round_idx, capacity)
+            rows.append(ret_ref[e % local, e // local, pl.ds(base, WIN), :])
+            slot = jnp.where(which == n, e * capacity + base, slot)
+            valid = jnp.where(which == n, e * capacity + first, valid)
+        slot = slot + inner
+        slot = jnp.where(slot >= valid, slot, -2).astype(jnp.float32)
+        picks = []
+        for k in range(2):
+            parts = [jnp.where(tok[:, k:k + 1] == slot[c:c + 1, :], 1.0, 0.0).astype(jnp.bfloat16) for c in range(width // lanes)]
+            picks.append(jnp.concatenate(parts, axis=1))
+        got = jnp.dot(jnp.concatenate(picks, axis=0), jnp.concatenate(rows, axis=0), preferred_element_type=jnp.float32)
+        return tok[:, 2:3] * got[:TILE] + tok[:, 3:4] * got[TILE:]
+
+    tiles = [pl.program_id(0) * SUB + n for n in range(SUB)]
+    spans = [slice(n * TILE, (n + 1) * TILE) for n in range(SUB)]
+    toks = [tok_ref[:, span].T for span in spans]
+    for tile, span, tok in zip(tiles, spans, toks):
+        out_ref[span, :] = (hidden_ref[span, :].astype(jnp.float32) + gathered(tile, tok, 0)).astype(out_ref.dtype)
+    for tile, span, tok in zip(tiles, spans, toks):
+        rounds = round_count(starts_ref, tile, experts, capacity)
+
+        @pl.when(rounds > 1)
+        def _():
+            total[...] = hidden_ref[span, :].astype(jnp.float32)
+
+            def more(round_idx, carry):
+                total[...] += gathered(tile, tok, round_idx)
+                return carry
+
+            lax.fori_loop(0, rounds, more, 0)
+            out_ref[span, :] = total[...].astype(out_ref.dtype)
+
+
+def combine(hidden, ret, tok, starts, capacity):
+    tok_count, d_model = hidden.shape
+    local, dests = ret.shape[:2]
     return pl.pallas_call(
-        functools.partial(combine_kernel, experts, local, capacity, len(rets)),
-        out_shape=jax.ShapeDtypeStruct(acc.shape, out_dtype),
+        functools.partial(combine_kernel, local, capacity),
+        out_shape=jax.ShapeDtypeStruct(hidden.shape, hidden.dtype),
         grid_spec=pltpu.PrefetchScalarGridSpec(
             num_scalar_prefetch=1,
-            grid=(tok_count // TILE,),
+            grid=(tok_count // (TILE * SUB),),
             in_specs=[
-                pl.BlockSpec((TILE, 4), lambda t, s: (t, 0)),
-                pl.BlockSpec((TILE, d_model), lambda t, s: (t, 0)),
-            ] + [pl.BlockSpec(shape, lambda t, s: (0, 0, 0, 0), pipeline_mode=pl.Buffered(1))] * len(rets),
-            out_specs=pl.BlockSpec((TILE, d_model), lambda t, s: (t, 0)),
-            scratch_shapes=[pltpu.VMEM((8 * WIN, d_model), jnp.bfloat16), pltpu.VMEM((TILE, d_model), jnp.float32)],
+                pl.BlockSpec((tok.shape[0], TILE * SUB), lambda t, s: (0, t)),
+                pl.BlockSpec((TILE * SUB, d_model), lambda t, s: (t, 0)),
+                pl.BlockSpec(ret.shape, lambda t, s: (0, 0, 0, 0), pipeline_mode=pl.Buffered(1)),
+            ],
+            out_specs=pl.BlockSpec((TILE * SUB, d_model), lambda t, s: (t, 0)),
+            scratch_shapes=[pltpu.VMEM((TILE, d_model), jnp.float32)],
         ),
         compiler_params=pltpu.CompilerParams(dimension_semantics=('arbitrary',), vmem_limit_bytes=VMEM_LIMIT),
-        cost_estimate=pl.CostEstimate(flops=4 * tok_count * len(experts) * WIN * d_model, bytes_accessed=8 * tok_count * d_model, transcendentals=0),
+        cost_estimate=pl.CostEstimate(flops=4 * tok_count * local * dests * WIN * d_model, bytes_accessed=8 * tok_count * d_model, transcendentals=0),
         name='combine_rows',
-    )(starts, tok, acc, *rets)
+    )(starts, tok, hidden, ret)
 
 
 class Unit(NamedTuple):
@@ -146,9 +125,9 @@
     return units
 
 
-def moe_kernel(units, capacity, slots_ref, normed_hbm, gate_hbm, up_hbm, down_hbm,
-               ret_hbm, send_hbm, recv_hbm, out_hbm, gate_all, up_all, down_all,
-               normed, stage, rows, act, wbuf, dbuf, obuf,
+def moe_kernel(units, capacity, ids_ref, gain_ref, router_ref, hidden_hbm, gate_hbm, up_hbm, down_hbm,
+               ret_hbm, tok_ref, starts_ref, send_hbm, recv_hbm, out_hbm, gate_all, up_all, down_all,
+               normed, slots_ref, stage, rows, act, wbuf, dbuf, obuf,
                w_send, w_recv, a_send, a_recv, r_send, r_recv, c_send, c_recv,
                normed_sem, stage_sem, rows_sem, wbuf_sem, dbuf_sem, obuf_sem):
     local, d_shard, ff = gate_hbm.shape
@@ -208,9 +187,49 @@
 
     for c in range(AHEAD):
         start_direct(c)
-    load = pltpu.make_async_copy(normed_hbm, normed, normed_sem)
+    load = pltpu.make_async_copy(hidden_hbm, normed, normed_sem)
     load.start()
     load.wait()
+    tok_count, d_model = normed.shape
+    num_experts = local * dests
+    gain = gain_ref[...].astype(jnp.float32)
+    expert_iota = lax.broadcasted_iota(jnp.int32, (num_experts, ROUTE), 0)
+    square = (ROUTE, ROUTE)
+    earlier = jnp.where(lax.broadcasted_iota(jnp.int32, square, 0) < lax.broadcasted_iota(jnp.int32, square, 1), 1.0, 0.0).astype(jnp.bfloat16)
+    tile_low = lax.broadcasted_iota(jnp.int32, (ROUTE, 128), 1) * TILE - lax.broadcasted_iota(jnp.int32, (ROUTE, 128), 0)
+
+    def route(block, carry):
+        seen, starts = carry
+        low = pl.multiple_of(block * ROUTE, ROUTE)
+        span = pl.ds(low, ROUTE)
+        x = normed[span, :].astype(jnp.float32)
+        mean_sq = jnp.mean(x * x, axis=-1, keepdims=True)
+        u = (x * lax.rsqrt(mean_sq + EPS) * gain).astype(jnp.bfloat16)
+        normed[span, :] = u
+        logits = lax.dot_general(router_ref[...], u, (((1,), (1,)), ((), ())), preferred_element_type=jnp.float32)
+        hits = [ids_ref[k:k + 1, span] == expert_iota for k in range(2)]
+        chosen = jnp.where(hits[0] | hits[1], 1.0, 0.0)
+        packed = chosen.astype(jnp.bfloat16)
+        rank = jnp.dot(packed, earlier, preferred_element_type=jnp.float32) + seen
+        keep = rank < capacity
+        slots_ref[:, span] = jnp.where((chosen > 0) & keep, rank, -1.0).astype(jnp.int32)
+        place = expert_iota.astype(jnp.float32) * capacity + rank + 1.0
+        picked = []
+        for k in range(2):
+            tok_ref[k:k + 1, span] = jnp.sum(jnp.where(hits[k] & keep, place, 0.0), axis=0, keepdims=True) - 1.0
+            picked.append(jnp.sum(jnp.where(hits[k], logits, 0.0), axis=0, keepdims=True))
+        top = jnp.maximum(picked[0], picked[1])
+        weights = [jnp.exp(p - top) for p in picked]
+        for k in range(2):
+            tok_ref[2 + k:3 + k, span] = weights[k] / (weights[0] + weights[1])
+        tok_ref[4:8, span] = jnp.zeros((4, ROUTE), jnp.float32)
+        before = jnp.where(tile_low > low, 1.0, 0.0).astype(jnp.bfloat16)
+        starts = starts + jnp.dot(packed, before, preferred_element_type=jnp.float32)
+        return seen + jnp.sum(chosen, axis=1, keepdims=True), starts
+
+    zero = (jnp.zeros((num_experts, 1), jnp.float32), jnp.zeros((num_experts, 128), jnp.float32))
+    _, starts = lax.fori_loop(0, tok_count // ROUTE, route, zero)
+    starts_ref[...] = jnp.minimum(starts, capacity).astype(jnp.int32)
 
     def dest_of(step):
         return lax.rem(j_me + 1 + step, dests)
@@ -227,11 +246,12 @@
 
     row_iota = lax.broadcasted_iota(jnp.int32, (capacity, normed.shape[0]), 0)
 
-    def dispatch(i):
-        def body(step, carry):
+    def dispatch(serve_at):
+        def body(s, carry):
+            i, step = s // dests, lax.rem(s, dests)
             want = slots_ref[pl.ds(dest_of(step) * local + i, 1), :]
             pick = jnp.where(row_iota == want, 1.0, 0.0).astype(jnp.bfloat16)
-            stage[lax.rem(step, 2)] = jnp.dot(pick, normed[...], preferred_element_type=jnp.float32).astype(jnp.bfloat16)
+            stage[lax.rem(s, 2)] = jnp.dot(pick, normed[...], preferred_element_type=jnp.float32).astype(jnp.bfloat16)
 
             @pl.when(step > 0)
             def _():
@@ -239,10 +259,16 @@
                 send_rows(i, step - 1).start()
 
             store_rows(i, step).start()
+
+            @pl.when(step == dests - 1)
+            def _():
+                store_rows(i, step).wait()
+
+            for at, act_on in serve_at.items():
+                pl.when(s == at)(act_on)
             return carry
 
-        lax.fori_loop(0, dests, body, 0)
-        store_rows(i, dests - 1).wait()
+        lax.fori_loop(0, local * dests, body, 0)
 
     def load_rows(e):
         def copy(step):
@@ -335,12 +361,15 @@
 
     def phase_two(e, far_unit):
         down_load(e, 0).start()
-        down_load(e, 1).start()
+        if e < last:
+            down_load(e, 1).start()
         down_load(e, 0).wait()
         down_column(e, 0)
         if e == last:
             for step in range(dests - 1):
                 back_cols(0, order[0], step).start()
+            serve(far_unit)
+            down_load(e, 1).start()
         down_load(e, 2).start()
         down_load(e, 1).wait()
         down_column(e, 1)
@@ -379,10 +408,7 @@
             service(done, then(done))
             done += 1
 
-    for i in range(local):
-        dispatch(i)
-        if i < local - 1:
-            serve(i)
+    dispatch({(i + 1) * dests - 1: functools.partial(serve, i) for i in range(local - 1)})
     blocks = ff // FFB
     for e in range(last):
         g = index[e, GATE, 0]
@@ -401,7 +427,6 @@
         wait_far(c + 1)
         low = units[c].low // FFB
         phase_one(last, low, low + units[c].size // FFB)
-    serve(final)
     phase_two(last, final)
 
     for e in range(last):
@@ -430,22 +455,26 @@
             back_cols(n, order[n], step).wait_send()
 
 
-def exchange(per_expert, normed, w_gate, w_up, w_down, fsdp, dests, capacity):
+def exchange(top2_ids, norm_gain, w_router, hidden, w_gate, w_up, w_down, fsdp, dests, capacity):
     local, d_shard, ff = w_gate.shape
-    tok_count, d_model = normed.shape
+    tok_count, d_model = hidden.shape
+    num_experts = w_router.shape[1]
     units = unit_list(local, ff)
     rows = (local, dests, capacity, d_model)
     bf16 = jnp.bfloat16
-    shapes = [rows, rows, rows, rows, (local, fsdp, d_shard, ff), (local, fsdp, d_shard, ff), (local, fsdp, ff, d_shard)]
+    shapes = [rows, rows, rows, (local, fsdp, d_shard, ff), (local, fsdp, d_shard, ff), (local, fsdp, ff, d_shard)]
     dma = pltpu.SemaphoreType.DMA
     anywhere = pl.BlockSpec(memory_space=pl.ANY)
+    vmem = pl.BlockSpec(memory_space=pltpu.VMEM)
     return pl.pallas_call(
         functools.partial(moe_kernel, units, capacity),
-        out_shape=[jax.ShapeDtypeStruct(s, bf16) for s in shapes],
-        in_specs=[pl.BlockSpec(memory_space=pltpu.VMEM)] + [anywhere] * 4,
-        out_specs=[anywhere] * len(shapes),
+        out_shape=[jax.ShapeDtypeStruct(rows, bf16), jax.ShapeDtypeStruct((8, tok_count), jnp.float32), jax.ShapeDtypeStruct((num_experts, 128), jnp.int32)]
+        + [jax.ShapeDtypeStruct(s, bf16) for s in shapes],
+        in_specs=[vmem] * 3 + [anywhere] * 4,
+        out_specs=[anywhere, vmem, vmem] + [anywhere] * len(shapes),
         scratch_shapes=[
             pltpu.VMEM((tok_count, d_model), bf16),
+            pltpu.VMEM((num_experts, tok_count), jnp.int32),
             pltpu.VMEM((2, capacity, d_model), bf16),
             pltpu.VMEM((dests, capacity, d_model), bf16),
             pltpu.VMEM((dests * capacity, ff), bf16),
@@ -460,19 +489,15 @@
         ],
         compiler_params=pltpu.CompilerParams(collective_id=0, has_side_effects=True, vmem_limit_bytes=VMEM_LIMIT),
         name='moe_exchange',
-    )(per_expert, normed, w_gate, w_up, w_down)[0]
+    )(top2_ids.T, norm_gain.reshape(1, d_model), w_router.T, hidden, w_gate, w_up, w_down)[:3]
 
 
 def local_block(hidden, norm_gain, w_router, w_gate, w_up, w_down, top2_ids, *, fsdp, dests):
-    tok_local, d_model = hidden.shape
+    tok_local = hidden.shape[0]
     num_experts = w_router.shape[1]
-    local = w_gate.shape[0]
     capacity = (5 * tok_local + 2 * num_experts - 1) // (2 * num_experts)
-    normed, gate_probs = norm_and_gates(hidden, norm_gain, w_router, top2_ids)
-    slots, per_expert, starts = route(top2_ids, num_experts, capacity)
-    tok = jnp.stack([slots[0].astype(jnp.float32), slots[1].astype(jnp.float32), gate_probs[:, 0], gate_probs[:, 1]], axis=1)
-    ret = exchange(per_expert, normed, w_gate, w_up, w_down, fsdp, dests, capacity)
-    return combine(hidden, [ret], list(range(local)), tok, starts, num_experts, capacity, local, jnp.bfloat16)
+    ret, tok, starts = exchange(top2_ids, norm_gain, w_router, hidden, w_gate, w_up, w_down, fsdp, dests, capacity)
+    return combine(hidden, ret, tok, starts, capacity)
 
 
 def solution(mesh):

time: 701 us -> 661 us (0.943)
  Pallas kernels: 674 us -> 659 us
  other arithmetic: 14.1 us -> 0 us
    pallas_call x1, Pallas kernels: 620 us -> 610 us  [exchange(): pl.pallas_call(functools.partial(moe_kernel, units, capacity), out_shape=...]
where the time goes in v2:
time: 661 us; the launch traced here: 660 us
  Pallas kernels  659 us (100%)
    pallas_call x1, Pallas kernels, exchange(): pl.pallas_call(functools.partial(moe_kernel, units, capacity), out_shape=...  610 us
    pallas_call x1, Pallas kernels, combine(): pl.pallas_call(functools.partial(combine_kernel, local, capacity), out_sh...  49.1 us

profile of v2, /device:TPU:97, one launch (start us, length us, event | category | flops | bytes accessed | tf_op | source)
XLA Modules:
  0.0 660.4 jit_solution(12896306303098451607)
XLA Ops:
  0.0 1.3 reshape.3.gain_ref
  1.3 610.1 %moe_exchange.1 = (bf16[4,8,320,1024]{3,2,1,0:T(8,128)(2,1)}, f32[8,4096]{1,0:T(8,128)}, s32[32,128]{1,0:T(8,128)}, bf16[4,8,320,1024]{3,2,1,0:T(8,128)(2,1)}, b...) custom-call(s32[2,4096]{1,0:T(2,128)} %bitcast.3, ...), custom_call_target="tpu_custom_call" | custom-call | tf_op jit(solution)/shard_map/moe_exchange/pallas_call | solution.py:469
  611.4 49.1 %combine_rows.1 = bf16[4096,1024]{1,0:T(8,128)(2,1)} custom-call(s32[32,128]{1,0:T(8,128)} %get-tuple-element.8.starts_ref, f32[8,4096]{1,0:T(8,128)} %get-tuple-element.9.tok_ref, bf16[4096,1024]{1,0:T(8,128)(2,1)} %hidden_ref.1, bf16[4,8,320,1024]{3,2,1,0:T(8,128)(2,1)} %get-tuple-element.10.ret_ref), custom_call_target="tpu_custom_call" | custom-call | flops 17179869184 | bytes 33554432 | tf_op jit(solution)/shard_map/combine_rows/pallas_call | solution.py:82

commit v3 on v2

--- a/solution.py
+++ b/solution.py
@@ -11,47 +11,24 @@
 EPS = 1e-5
 TILE = 128
 WIN = 32
-SUB = 1
+SUB = 2
 ALIGN = 8
 ROUTE = 512
 VMEM_LIMIT = 60 * 1024 * 1024
 
 
-def window(starts_ref, tile, expert, round_idx, capacity):
-    first = starts_ref[expert, tile] // ALIGN * ALIGN + round_idx * WIN
-    base = jnp.minimum(first, capacity - WIN)
-    return pl.multiple_of(base, ALIGN), first
-
-
-def round_count(starts_ref, tile, experts, capacity):
-    need = jnp.int32(0)
-    for expert in experts:
-        low = starts_ref[expert, tile] // ALIGN * ALIGN
-        need = jnp.maximum(need, starts_ref[expert, tile + 1] - low)
-    return (need + WIN - 1) // WIN
-
-
-def combine_kernel(local, capacity, starts_ref, tok_ref, hidden_ref, ret_ref, out_ref, total):
+ROUNDS, FIRSTS = 32, 40
+
+
+def combine_kernel(local, capacity, plan_ref, tok_ref, slot_ref, hidden_ref, ret_ref, out_ref, total):
     dests = ret_ref.shape[1]
     experts = [j * local + i for i in range(local) for j in range(dests)]
     width, lanes = len(experts) * WIN, 128
-    spot = lax.broadcasted_iota(jnp.int32, (width // lanes, lanes), 0) * lanes + lax.broadcasted_iota(jnp.int32, (width // lanes, lanes), 1)
-    which, inner = spot // WIN, spot % WIN
-
-    def gathered(tile, tok, round_idx):
-        slot = jnp.zeros(spot.shape, jnp.int32)
-        valid = jnp.zeros(spot.shape, jnp.int32)
-        rows = []
-        for n, e in enumerate(experts):
-            base, first = window(starts_ref, tile, e, round_idx, capacity)
-            rows.append(ret_ref[e % local, e // local, pl.ds(base, WIN), :])
-            slot = jnp.where(which == n, e * capacity + base, slot)
-            valid = jnp.where(which == n, e * capacity + first, valid)
-        slot = slot + inner
-        slot = jnp.where(slot >= valid, slot, -2).astype(jnp.float32)
+
+    def picked(tok, slots, rows):
         picks = []
         for k in range(2):
-            parts = [jnp.where(tok[:, k:k + 1] == slot[c:c + 1, :], 1.0, 0.0).astype(jnp.bfloat16) for c in range(width // lanes)]
+            parts = [jnp.where(tok[:, k:k + 1] == slots[c], 1.0, 0.0).astype(jnp.bfloat16) for c in range(width // lanes)]
             picks.append(jnp.concatenate(parts, axis=1))
         got = jnp.dot(jnp.concatenate(picks, axis=0), jnp.concatenate(rows, axis=0), preferred_element_type=jnp.float32)
         return tok[:, 2:3] * got[:TILE] + tok[:, 3:4] * got[TILE:]
@@ -60,43 +37,62 @@
     spans = [slice(n * TILE, (n + 1) * TILE) for n in range(SUB)]
     toks = [tok_ref[:, span].T for span in spans]
     for tile, span, tok in zip(tiles, spans, toks):
-        out_ref[span, :] = (hidden_ref[span, :].astype(jnp.float32) + gathered(tile, tok, 0)).astype(out_ref.dtype)
+        rows = [ret_ref[e % local, e // local, pl.ds(pl.multiple_of(plan_ref[tile, e], ALIGN), WIN), :] for e in experts]
+        line = slot_ref[pl.ds(lax.rem(tile, 8), 1), :]
+        slots = [line[:, c * lanes:(c + 1) * lanes] for c in range(width // lanes)]
+        out_ref[span, :] = (hidden_ref[span, :].astype(jnp.float32) + picked(tok, slots, rows)).astype(out_ref.dtype)
+
+    spot = lax.broadcasted_iota(jnp.int32, (width // lanes, lanes), 0) * lanes + lax.broadcasted_iota(jnp.int32, (width // lanes, lanes), 1)
+    which, inner = spot // WIN, spot % WIN
     for tile, span, tok in zip(tiles, spans, toks):
-        rounds = round_count(starts_ref, tile, experts, capacity)
+        rounds = plan_ref[tile, ROUNDS]
 
         @pl.when(rounds > 1)
         def _():
             total[...] = hidden_ref[span, :].astype(jnp.float32)
 
             def more(round_idx, carry):
-                total[...] += gathered(tile, tok, round_idx)
+                slot = jnp.zeros(spot.shape, jnp.int32)
+                valid = jnp.zeros(spot.shape, jnp.int32)
+                rows = []
+                for n, e in enumerate(experts):
+                    first = plan_ref[tile, FIRSTS + e] + round_idx * WIN
+                    base = pl.multiple_of(jnp.minimum(first, capacity - WIN), ALIGN)
+                    rows.append(ret_ref[e % local, e // local, pl.ds(base, WIN), :])
+                    slot = jnp.where(which == n, e * capacity + base, slot)
+                    valid = jnp.where(which == n, e * capacity + first, valid)
+                slot = slot + inner
+                slot = jnp.where(slot >= valid, slot, -2).astype(jnp.float32)
+                total[...] += picked(tok, [slot[c:c + 1, :] for c in range(width // lanes)], rows)
                 return carry
 
             lax.fori_loop(0, rounds, more, 0)
             out_ref[span, :] = total[...].astype(out_ref.dtype)
 
 
-def combine(hidden, ret, tok, starts, capacity):
+def combine(hidden, ret, tok, plan, slots, capacity):
     tok_count, d_model = hidden.shape
     local, dests = ret.shape[:2]
+    step = TILE * SUB
     return pl.pallas_call(
         functools.partial(combine_kernel, local, capacity),
         out_shape=jax.ShapeDtypeStruct(hidden.shape, hidden.dtype),
         grid_spec=pltpu.PrefetchScalarGridSpec(
             num_scalar_prefetch=1,
-            grid=(tok_count // (TILE * SUB),),
+            grid=(tok_count // step,),
             in_specs=[
-                pl.BlockSpec((tok.shape[0], TILE * SUB), lambda t, s: (0, t)),
-                pl.BlockSpec((TILE * SUB, d_model), lambda t, s: (t, 0)),
+                pl.BlockSpec((tok.shape[0], step), lambda t, s: (0, t)),
+                pl.BlockSpec((8, slots.shape[1]), lambda t, s: (t * SUB // 8, 0)),
+                pl.BlockSpec((step, d_model), lambda t, s: (t, 0)),
                 pl.BlockSpec(ret.shape, lambda t, s: (0, 0, 0, 0), pipeline_mode=pl.Buffered(1)),
             ],
-            out_specs=pl.BlockSpec((TILE * SUB, d_model), lambda t, s: (t, 0)),
+            out_specs=pl.BlockSpec((step, d_model), lambda t, s: (t, 0)),
             scratch_shapes=[pltpu.VMEM((TILE, d_model), jnp.float32)],
         ),
         compiler_params=pltpu.CompilerParams(dimension_semantics=('arbitrary',), vmem_limit_bytes=VMEM_LIMIT),
         cost_estimate=pl.CostEstimate(flops=4 * tok_count * local * dests * WIN * d_model, bytes_accessed=8 * tok_count * d_model, transcendentals=0),
         name='combine_rows',
-    )(starts, tok, hidden, ret)
+    )(plan, tok, slots, hidden, ret)
 
 
 class Unit(NamedTuple):
@@ -126,7 +122,7 @@
 
 
 def moe_kernel(units, capacity, ids_ref, gain_ref, router_ref, hidden_hbm, gate_hbm, up_hbm, down_hbm,
-               ret_hbm, tok_ref, starts_ref, send_hbm, recv_hbm, out_hbm, gate_all, up_all, down_all,
+               ret_hbm, tok_ref, plan_ref, line_ref, send_hbm, recv_hbm, out_hbm, gate_all, up_all, down_all,
                normed, slots_ref, stage, rows, act, wbuf, dbuf, obuf,
                w_send, w_recv, a_send, a_recv, r_send, r_recv, c_send, c_recv,
                normed_sem, stage_sem, rows_sem, wbuf_sem, dbuf_sem, obuf_sem):
@@ -199,7 +195,7 @@
     tile_low = lax.broadcasted_iota(jnp.int32, (ROUTE, 128), 1) * TILE - lax.broadcasted_iota(jnp.int32, (ROUTE, 128), 0)
 
     def route(block, carry):
-        seen, starts = carry
+        seen, starts, ends = carry
         low = pl.multiple_of(block * ROUTE, ROUTE)
         span = pl.ds(low, ROUTE)
         x = normed[span, :].astype(jnp.float32)
@@ -223,13 +219,30 @@
         for k in range(2):
             tok_ref[2 + k:3 + k, span] = weights[k] / (weights[0] + weights[1])
         tok_ref[4:8, span] = jnp.zeros((4, ROUTE), jnp.float32)
-        before = jnp.where(tile_low > low, 1.0, 0.0).astype(jnp.bfloat16)
-        starts = starts + jnp.dot(packed, before, preferred_element_type=jnp.float32)
-        return seen + jnp.sum(chosen, axis=1, keepdims=True), starts
-
-    zero = (jnp.zeros((num_experts, 1), jnp.float32), jnp.zeros((num_experts, 128), jnp.float32))
-    _, starts = lax.fori_loop(0, tok_count // ROUTE, route, zero)
-    starts_ref[...] = jnp.minimum(starts, capacity).astype(jnp.int32)
+        before = [jnp.where(tile_low + n * TILE > low, 1.0, 0.0).astype(jnp.bfloat16) for n in range(2)]
+        starts = starts + jnp.dot(packed, before[0], preferred_element_type=jnp.float32)
+        ends = ends + jnp.dot(packed, before[1], preferred_element_type=jnp.float32)
+        return seen + jnp.sum(chosen, axis=1, keepdims=True), starts, ends
+
+    counts = jnp.zeros((num_experts, 128), jnp.float32)
+    _, starts, ends = lax.fori_loop(0, tok_count // ROUTE, route, (jnp.zeros((num_experts, 1), jnp.float32), counts, counts))
+    eighths = jnp.minimum(starts, capacity).astype(jnp.int32) // ALIGN
+    bases = jnp.minimum(eighths, (capacity - WIN) // ALIGN)
+    need = jnp.max(jnp.minimum(ends, capacity).astype(jnp.int32) - eighths * ALIGN, axis=0, keepdims=True)
+    rounds = jnp.broadcast_to((need + WIN - 1) // WIN, (8, 128))
+    blank = jnp.zeros((128 - 8 - 2 * num_experts, 128), jnp.int32)
+    plan = jnp.concatenate([bases * ALIGN, rounds, eighths * ALIGN, blank], axis=0).astype(jnp.float32).T
+    tiles, width = line_ref.shape
+    plan_ref[...] = plan[:tiles].astype(jnp.int32)
+    spot = lax.broadcasted_iota(jnp.int32, (128, width), 1)
+    source = lax.broadcasted_iota(jnp.int32, (128, width), 0)
+    which = spot // WIN
+    owner = lax.rem(which, dests) * local + which // dests
+    spread = [jnp.where(source == owner + n * FIRSTS, 1.0, 0.0).astype(jnp.bfloat16) for n in range(2)]
+    scaled = (plan[:tiles] * (1.0 / ALIGN)).astype(jnp.bfloat16)
+    base, first = [jnp.dot(scaled, m, preferred_element_type=jnp.float32) * ALIGN for m in spread]
+    inner = (spot - which * WIN)[:tiles].astype(jnp.float32)
+    line_ref[...] = jnp.where(base + inner >= first, owner[:tiles].astype(jnp.float32) * capacity + base + inner, -2.0)
 
     def dest_of(step):
         return lax.rem(j_me + 1 + step, dests)
@@ -468,10 +481,10 @@
     vmem = pl.BlockSpec(memory_space=pltpu.VMEM)
     return pl.pallas_call(
         functools.partial(moe_kernel, units, capacity),
-        out_shape=[jax.ShapeDtypeStruct(rows, bf16), jax.ShapeDtypeStruct((8, tok_count), jnp.float32), jax.ShapeDtypeStruct((num_experts, 128), jnp.int32)]
+        out_shape=[jax.ShapeDtypeStruct(rows, bf16), jax.ShapeDtypeStruct((8, tok_count), jnp.float32), jax.ShapeDtypeStruct((tok_count // TILE, 128), jnp.int32), jax.ShapeDtypeStruct((tok_count // TILE, num_experts * WIN), jnp.float32)]
         + [jax.ShapeDtypeStruct(s, bf16) for s in shapes],
         in_specs=[vmem] * 3 + [anywhere] * 4,
-        out_specs=[anywhere, vmem, vmem] + [anywhere] * len(shapes),
+        out_specs=[anywhere, vmem, vmem, vmem] + [anywhere] * len(shapes),
         scratch_shapes=[
             pltpu.VMEM((tok_count, d_model), bf16),
             pltpu.VMEM((num_experts, tok_count), jnp.int32),
@@ -489,15 +502,15 @@
         ],
         compiler_params=pltpu.CompilerParams(collective_id=0, has_side_effects=True, vmem_limit_bytes=VMEM_LIMIT),
         name='moe_exchange',
-    )(top2_ids.T, norm_gain.reshape(1, d_model), w_router.T, hidden, w_gate, w_up, w_down)[:3]
+    )(top2_ids.T, norm_gain.reshape(1, d_model), w_router.T, hidden, w_gate, w_up, w_down)[:4]
 
 
 def local_block(hidden, norm_gain, w_router, w_gate, w_up, w_down, top2_ids, *, fsdp, dests):
     tok_local = hidden.shape[0]
     num_experts = w_router.shape[1]
     capacity = (5 * tok_local + 2 * num_experts - 1) // (2 * num_experts)
-    ret, tok, starts = exchange(top2_ids, norm_gain, w_router, hidden, w_gate, w_up, w_down, fsdp, dests, capacity)
-    return combine(hidden, ret, tok, starts, capacity)
+    ret, tok, plan, slots = exchange(top2_ids, norm_gain, w_router, hidden, w_gate, w_up, w_down, fsdp, dests, capacity)
+    return combine(hidden, ret, tok, plan, slots, capacity)
 
 
 def solution(mesh):

time: 661 us -> 646 us (0.977)
  Pallas kernels: 659 us -> 644 us
    pallas_call x1, Pallas kernels: 49.1 us -> 34 us  [combine(): pl.pallas_call(functools.partial(combine_kernel, local, capacity), out_sh...]
where the time goes in v3:
time: 646 us; the launch traced here: 645 us
  Pallas kernels  644 us (100%)
    pallas_call x1, Pallas kernels, exchange(): pl.pallas_call(functools.partial(moe_kernel, units, capacity), out_shape=...  610 us
    pallas_call x1, Pallas kernels, combine(): pl.pallas_call(functools.partial(combine_kernel, local, capacity), out_sh...  34 us

profile of v3, /device:TPU:97, one launch (start us, length us, event | category | flops | bytes accessed | tf_op | source)
XLA Modules:
  0.0 645.3 jit_solution(14862829519368627715)
XLA Ops:
  0.0 1.3 reshape.3.gain_ref
  1.3 610.1 %moe_exchange.1 = (bf16[4,8,320,1024]{3,2,1,0:T(8,128)(2,1)}, f32[8,4096]{1,0:T(8,128)}, s32[32,128]{1,0:T(8,128)}, f32[32,1024]{1,0:T(8,128)}, bf16[4,8,320,102...) custom-call(s32[2,4096]{1,0:T(2,128)} %bitcast.3, ...), custom_call_target="tpu_custom_call" | custom-call | tf_op jit(solution)/shard_map/moe_exchange/pallas_call | solution.py:482
  611.4 34.0 %combine_rows.1 = bf16[4096,1024]{1,0:T(8,128)(2,1)} custom-call(s32[32,128]{1,0:T(8,128)} %get-tuple-element.9.plan_ref, f32[8,4096]{1,0:T(8,128)} %get-tuple-element.10.tok_ref, f32[32,1024]{1,0:T(8,128)} %get-tuple-element.11.slot_ref, bf16[4096,1024]{1,0:T(8,128)(2,1)} %hidden_ref.1, bf16[4,8,320,1024]{3,2,1,0:T(8,128)(2,1)} %get-tuple-element.12.ret_ref), custom_call_target="tpu_custom_call" | custom-call | flops 17179869184 | bytes 33554432 | tf_op jit(solution)/shard_map/combine_rows/pallas_call | solution.py:77
